TPU v7x, 32 devices: a whole 2x2x4 slice. The times are simulated.
32 devices in a mesh: dp: 2 (over x), tp: 4 (over z), section: 4 (over y, core).
Axes of the slice: x: 2, y: 2, z: 4, core: 2. Of those that a mesh axis runs over, the one named last changes fastest.
Arguments:
- tokens: bfloat16 [256, 2304], P('dp', 'section'), may hold values from -6 to 6
- hidden_grad: bfloat16 [256, 18432], P('dp', ('tp', 'section')), may hold values from -6 to 6
- norm_gain: float32 [2304], replicated, may hold values from 0.5 to 1.5
- w_gate: bfloat16 [2304, 18432], P('dp', ('tp', 'section')), may hold values from -0.125 to 0.125
- w_up: bfloat16 [2304, 18432], P('dp', ('tp', 'section')), may hold values from -0.125 to 0.125
Outputs:
- grad_tokens: bfloat16 [256, 2304], P('dp', ('tp', 'section'))
- grad_gain: float32 [2304], P(('tp', 'section'))
- grad_gate: bfloat16 [2304, 18432], P('dp', ('tp', 'section'))
- grad_up: bfloat16 [2304, 18432], P('dp', ('tp', 'section'))
All inputs are finite; a program needn't handle non-finite values.
Results may differ from a plain program's by a relative error of at most 0.018.
Values may be sent and summed in bfloat16 or wider, within the bound.
A program may use at most 128 MiB of HBM per device.

v0:
```python
import jax
import jax.numpy as jnp
from jax import lax
from jax.sharding import PartitionSpec as P

D = 2304
epsilon = 1e-06


def gated_unit(gate, up):
    return jax.nn.gelu(gate, approximate=True) * up


def shards(tokens, hidden_grad, norm_gain, w_gate, w_up):
    n_dp = lax.axis_size("dp")
    n_model = lax.axis_size(("tp", "section"))
    rows_in = lax.all_gather(tokens, "section", axis=1, tiled=True)
    inputs = rows_in.astype(jnp.float32)
    inv_rms = lax.rsqrt(jnp.mean(inputs * inputs, axis=1) + epsilon)
    normed = (inputs * inv_rms[:, None] * norm_gain).astype(jnp.bfloat16)
    per_device, features = normed.shape
    cols_normed = lax.all_to_all(normed, "dp", split_axis=1, concat_axis=0, tiled=True)
    width = w_gate.shape[1]
    part_gate = jnp.dot(cols_normed, w_gate, preferred_element_type=jnp.float32)
    part_up = jnp.dot(cols_normed, w_up, preferred_element_type=jnp.float32)
    parts = jnp.concatenate([part_gate, part_up], axis=1).astype(jnp.bfloat16)
    parts = lax.all_to_all(parts, "dp", split_axis=0, concat_axis=0, tiled=True)
    sums = jnp.sum(parts.reshape(n_dp, per_device, 2 * width).astype(jnp.float32), axis=0)
    gate, up = (sums[:, :width], sums[:, width:])
    hidden, pull = jax.vjp(gated_unit, gate, up)
    d_both = jnp.concatenate(pull(hidden_grad.astype(jnp.float32)), axis=1).astype(jnp.bfloat16)
    d_all = lax.all_gather(d_both, "dp", axis=0, tiled=True)
    d_gate, d_up = (d_all[:, :width], d_all[:, width:])
    contract_cols = (((1,), (1,)), ((), ()))
    contract_rows = (((0,), (0,)), ((), ()))
    first = lax.dot_general(w_gate, d_gate, contract_cols, preferred_element_type=jnp.float32)
    second = lax.dot_general(w_up, d_up, contract_cols, preferred_element_type=jnp.float32)
    own_width = features // n_model
    per_row = n_model // n_dp
    d_part = (first + second).astype(jnp.bfloat16)
    d_part = d_part.reshape(per_row, own_width, n_dp, per_device).transpose(2, 0, 1, 3)
    d_part = d_part.reshape(n_model * own_width, per_device)
    d_columns = lax.psum_scatter(d_part, ("tp", "section"), scatter_dimension=0, tiled=True)
    moves = [
        (i * n_model + o * per_row + r, o * n_model + i * per_row + r)
        for i in range(n_dp)
        for o in range(n_dp)
        for r in range(per_row)
    ]
    d_columns = lax.ppermute(d_columns, ("dp", "tp", "section"), moves)
    d_normed = d_columns.astype(jnp.float32).T
    offset = lax.axis_index(("tp", "section")) * own_width
    own_inputs = lax.dynamic_slice_in_dim(inputs, offset, own_width, 1)
    own_gain = lax.dynamic_slice_in_dim(norm_gain, offset, own_width, 0)
    gain_part = jnp.sum(d_normed * own_inputs * inv_rms[:, None], axis=0)
    row_part = jnp.sum(own_inputs * own_gain * d_normed, axis=1)
    grad_gain = lax.psum(gain_part, "dp")
    row_sum = lax.psum(row_part, ("tp", "section"))
    grad_tokens = (
        inv_rms[:, None] * own_gain * d_normed
        - own_inputs * (inv_rms**3 * row_sum / features)[:, None]
    )
    grad_gate = lax.dot_general(
        cols_normed, d_gate, contract_rows, preferred_element_type=jnp.float32
    )
    grad_up = lax.dot_general(cols_normed, d_up, contract_rows, preferred_element_type=jnp.float32)
    return (
        grad_tokens.astype(jnp.bfloat16),
        grad_gain,
        grad_gate.astype(jnp.bfloat16),
        grad_up.astype(jnp.bfloat16),
    )


def solution(mesh):
    in_specs = (
        P("dp", "section"),
        P("dp", ("tp", "section")),
        P(),
        P("dp", ("tp", "section")),
        P("dp", ("tp", "section")),
    )
    out_specs = (
        P("dp", ("tp", "section")),
        P(("tp", "section")),
        P("dp", ("tp", "section")),
        P("dp", ("tp", "section")),
    )
    return jax.shard_map(shards, mesh=mesh, in_specs=in_specs, out_specs=out_specs, check_vma=False)
```

profile of v0, /device:TPU:0, one launch (start us, length us, event | category | flops | bytes accessed | tf_op | source)
XLA Modules:
  0.0 196.5 jit_solution(1719906381612836004)
XLA Ops:
  7.2 0.0 copy-start
  7.2 0.0 copy-start.5
  7.2 0.0 all-gather.2.cloned.1.call-start
  7.2 9.4 %all_gather.6 = bf16[128,2304]{0,1:T(8,128)(2,1)S(1)} all-gather(bf16[128,576]{0,1:T(8,128)(2,1)} %param.5), channel_id=1, replica_groups=mesh['dp'=2,'tp'=4,'section'=4] {'section'}, dimensions={1}, use_global_device_ids=true | all-gather | bytes 737280 | tf_op jit(solution)/shard_map/all_gather | solution.py:17
  16.6 0.3 multiply_reduce_fusion
  16.9 0.0 copy-done.5
  16.9 1.2 multiply_convert_fusion
  18.1 2.1 %copy.10 = bf16[128,2,1152]{2,0,1:T(8,128)(2,1)} copy(bf16[128,2,1152]{0,2,1:T(8,128)(2,1)} %bitcast.44) | data formatting | bytes 1179648 | tf_op jit(solution)/shard_map/all_to_all | solution.py:22
  20.3 13.0 %all_to_all.25 = bf16[128,2,1152]{2,0,1:T(8,128)(2,1)S(1)} all-to-all(bf16[128,2,1152]{2,0,1:T(8,128)(2,1)} %copy.10), channel_id=1, replica_groups=mesh['dp'=2,'tp'=4,'section'=4] {'dp'}, dimensions={1} | all-to-all | bytes 1179648 | tf_op jit(solution)/shard_map/all_to_all | solution.py:22
  33.2 0.0 copy-start.1
  33.2 3.0 %fusion.7 = bf16[2,128,1152]{2,1,0:T(8,128)(2,1)S(1)} fusion(bf16[1152,1152]{1,0:T(8,128)(2,1)} %param.9, bf16[128,2,1152]{2,0,1:T(8,128)(2,1)S(1)} %all_to_all.25), kind=kOutput, calls=%fused_computation.8 | convolution fusion | flops 679772160 | bytes 3833856 | tf_op jit(solution)/shard_map/dot_general | solution.py:25
  36.2 0.0 copy-done.1
  36.2 0.0 copy-done
  36.2 1.0 fusion.4
  37.2 0.1 pad_maximum_fusion
  37.3 17.4 %all_to_all.26 = bf16[2,128,2304]{2,1,0:T(8,128)(2,1)S(1)} all-to-all(bf16[2,128,2304]{2,1,0:T(8,128)(2,1)S(1)} %pad_maximum_fusion), channel_id=1, replica_groups=mesh['dp'=2,'tp'=4,'section'=4] {'dp'}, dimensions={0} | all-to-all | bytes 2359296 | tf_op jit(solution)/shard_map/all_to_all | solution.py:27
  54.7 0.0 copy-start.4
  54.7 0.2 convert_reduce_fusion
  54.9 0.8 copy-done.4
  55.7 0.5 fusion.19
  56.2 0.9 pad_maximum_fusion.1
  57.0 0.0 all-gather.2.cloned.1.call-update
  57.0 0.0 reduce-scatter.2.cloned.1.call-start
  57.1 22.7 %all-gather.2.cloned.1.call-done = bf16[256,2304]{1,0:T(8,128)(2,1)} async-done(((bf16[128,2304]{1,0:T(8,128)(2,1)}), bf16[256,2304]{1,0:T(8,128)(2,1)}) %all-gather.2.cloned.1.call-update) | async-done | bytes 1179664 | tf_op jit(solution)/shard_map/all_gather | solution.py:32
  79.8 0.0 copy-start.3
  79.8 0.0 copy-start.6
  79.8 2.2 %fusion.25 = f32[256,1152]{1,0:T(8,128)S(1)} fusion(bf16[1152,1152]{1,0:T(8,128)(2,1)S(1)} %copy-done, bf16[256,2304]{1,0:T(8,128)(2,1)} %all-gather.2.cloned.1.call-done), kind=kOutput, calls=%fused_computation.33 | convolution fusion | flops 679477248 | bytes 4423680 | tf_op jit(solution)/shard_map/dot_general | solution.py:36
  82.1 0.0 copy-done.3
  82.1 0.0 copy-done.6
  82.1 1.9 fusion.11
  84.0 2.1 %copy.11 = bf16[1152,256]{1,0:T(8,128)(2,1)} copy(bf16[1152,256]{0,1:T(8,128)(2,1)} %fusion.11) | data formatting | bytes 1179648 | tf_op jit(solution)/shard_map/convert_element_type | solution.py:40
  86.1 2.5 %reshape.35 = bf16[8,144,2,128]{3,2,1,0:T(2,128)(2,1)} reshape(bf16[1152,256]{1,0:T(8,128)(2,1)} %copy.11) | data formatting | bytes 1179648 | tf_op jit(solution)/shard_map/reshape | solution.py:41
  88.6 2.0 copy.12
  90.5 0.0 reduce-scatter.2.cloned.1.call-update
  90.5 1.1 convert_element_type.31
  91.7 0.1 dynamic_slice.6
  91.7 0.0 copy-start.2
  91.7 3.8 %convolution_convert_fusion.1 = bf16[1152,1152]{1,0:T(8,128)(2,1)} fusion(bf16[256,1152]{1,0:T(8,128)(2,1)} %bitcast.40, bf16[256,2304]{1,0:T(8,128)(2,1)} %all-gather.2.cloned.1.call-done), kind=kOutput, calls=%fused_computation.1 | convolution fusion | flops 680804352 | bytes 3833856 | tf_op jit(solution)/shard_map/dot_general | solution.py:63
  95.5 49.3 %reduce-scatter.2.cloned.1.call-done = bf16[144,128]{1,0:T(8,128)(2,1)} async-done(((bf16[2304,128]{1,0:T(8,128)(2,1)}), bf16[144,128]{1,0:T(8,128)(2,1)}) %reduce-scatter.2.cloned.1.call-update) | async-done | bytes 36880 | tf_op jit(solution)/shard_map/reduce_scatter | solution.py:43
  144.8 1.4 collective-permute-start
  146.2 0.0 copy-done.2
  146.2 3.6 %convolution_convert_fusion = bf16[1152,1152]{1,0:T(8,128)(2,1)} fusion(bf16[256,1152]{1,0:T(8,128)(2,1)S(1)} %bitcast.41, bf16[256,2304]{1,0:T(8,128)(2,1)} %all-gather.2.cloned.1.call-done), kind=kOutput, calls=%fused_computation | convolution fusion | flops 680804352 | bytes 3833856 | tf_op jit(solution)/shard_map/dot_general | solution.py:66
  149.8 0.0 collective-permute-done
  149.8 1.0 fusion.31
  150.8 7.8 %psum.15 = f32[144]{0:T(256)} all-reduce(f32[144]{0:T(256)S(1)} %get-tuple-element.4), channel_id=1, replica_groups=mesh['dp'=2,'tp'=4,'section'=4] {'dp'}, use_global_device_ids=true, to_apply=%region_6.0 | all-reduce | flops 144 | bytes 1152 | tf_op jit(solution)/shard_map/psum | solution.py:57
  158.6 29.5 %psum.14 = f32[128]{0:T(128)S(1)} all-reduce(f32[128]{0:T(128)S(1)} %get-tuple-element.5), channel_id=1, replica_groups=mesh['dp'=2,'tp'=4,'section'=4] {'tp','section'}, use_global_device_ids=true, to_apply=%region_4.0 | all-reduce | flops 128 | bytes 1024 | tf_op jit(solution)/shard_map/psum | solution.py:58
  188.1 1.6 fusion.28
  (2 shorter events, 0.0 us)
Async XLA Ops:
  7.2 29.0 %copy-start = (bf16[1152,1152]{1,0:T(8,128)(2,1)S(1)}, bf16[1152,1152]{1,0:T(8,128)(2,1)}, u32[]{:S(2)}) copy-start(bf16[1152,1152]{1,0:T(8,128)(2,1)} %param.8) | copy-start | bytes 7962628
  7.2 9.8 %copy-start.5 = (f32[2304]{0:T(1024)S(1)}, f32[2304]{0:T(1024)}, u32[]{:S(2)}) copy-start(f32[2304]{0:T(1024)} %param.7) | copy-start | bytes 27652
  7.2 72.6 %all-gather.2.cloned.1.call-start = ((), (), s32[]{:S(2)}) async-start(), calls=%async_computation.3 | async-start | bytes 1769472 | tf_op jit(solution)/shard_map/all_gather | solution.py:32
  33.2 3.0 %copy-start.1 = (bf16[128,2,1152]{2,0,1:T(8,128)(2,1)}, bf16[128,2,1152]{2,0,1:T(8,128)(2,1)S(1)}, u32[]{:S(2)}) copy-start(bf16[128,2,1152]{2,0,1:T(8,128)(2,1)S(1)} %all_to_all.25) | copy-start | bytes 1769476
  54.7 1.0 copy-start.4
  57.0 87.8 %reduce-scatter.2.cloned.1.call-start = ((), (), s32[]{:S(2)}) async-start(), calls=%async_computation.4 | async-start | bytes 626688 | tf_op jit(solution)/shard_map/reduce_scatter | solution.py:43
  79.8 2.3 %copy-start.3 = (bf16[256,2304]{1,0:T(8,128)(2,1)S(1)}, bf16[256,2304]{1,0:T(8,128)(2,1)}, u32[]{:S(2)}) copy-start(bf16[256,2304]{1,0:T(8,128)(2,1)} %all-gather.2.cloned.1.call-done) | copy-start | bytes 3538948
  79.8 2.3 %copy-start.6 = (bf16[1152,1152]{1,0:T(8,128)(2,1)S(1)}, bf16[1152,1152]{1,0:T(8,128)(2,1)}, u32[]{:S(2)}) copy-start(bf16[1152,1152]{1,0:T(8,128)(2,1)} %param.9) | copy-start | bytes 7962628
  91.7 54.5 %copy-start.2 = (bf16[128,2,1152]{2,0,1:T(8,128)(2,1)S(1)}, bf16[128,2,1152]{2,0,1:T(8,128)(2,1)}, u32[]{:S(2)}) copy-start(bf16[128,2,1152]{2,0,1:T(8,128)(2,1)} %copy-done.1) | copy-start | bytes 1769476
  144.8 5.0 %collective-permute-start = (bf16[144,128]{1,0:T(8,128)(2,1)}, bf16[144,128]{1,0:T(8,128)(2,1)S(1)}, u32[]{:S(2)}, u32[]{:S(2)}) collective-permute-start(bf16[144,128]{1,0:T(8,128)(2,1)} %reduce-scatter.2.cloned.1.call-done), channel_id=1, source_target_pairs={{0,0},{1,1},{2,2},{3,3},{4,4},{5,5},{6,6},{7,7},{8,16},{9,17},{10,... | collective-permute-start | bytes 110600 | tf_op jit(solution)/shard_map/ppermute | solution.py:50
Sparse Core Ops, SparseCore 0:
  57.2 22.6 all-gather.1
  90.7 54.0 reduce-scatter.1
where the time goes:
time: 197 us
  blocking collectives  77 us (39%)
  waiting for transfers between devices  72 us (37%)
  matrix products  15.4 us (8%)
  between operations  14.1 us (7%)
  local copies, waits for them, and re-layouts  9.56 us (5%)
  other arithmetic  6.9 us (4%)
    reduce_scatter x1, waiting for transfers between devices, shards(): lax.psum_scatter(d_part, ('tp', 'section'), scatter_dimension=0, tiled=True)  49.3 us
    psum x1, blocking collectives, shards(): row_sum = lax.psum(row_part, ('tp', 'section'))  29.5 us
    all_gather x1, waiting for transfers between devices, shards(): d_all = lax.all_gather(d_both, 'dp', axis=0, tiled=True)  22.7 us
    all_to_all x1, blocking collectives, shards(): parts = lax.all_to_all(parts, 'dp', split_axis=0, concat_axis=0, tiled=True)  17.4 us
    all_to_all x1, blocking collectives, shards(): lax.all_to_all(normed, 'dp', split_axis=1, concat_axis=0, tiled=True)  13 us
    all_gather x1, blocking collectives, shards(): rows_in = lax.all_gather(tokens, 'section', axis=1, tiled=True)  9.38 us
    psum x1, blocking collectives, shards(): grad_gain = lax.psum(gain_part, 'dp')  7.8 us
  transfers between devices with their start and end apart: 3, of which 2 were waited for; matrix products, arithmetic and copies ran while one was open for 4% of the time, Pallas kernels for 0%

commit v1 on v0

--- a/solution.py
+++ b/solution.py
@@ -55,7 +55,7 @@
     gain_part = jnp.sum(d_normed * own_inputs * inv_rms[:, None], axis=0)
     row_part = jnp.sum(own_inputs * own_gain * d_normed, axis=1)
     grad_gain = lax.psum(gain_part, "dp")
-    row_sum = lax.psum(row_part, ("tp", "section"))
+    row_sum = jnp.sum(jax.lax.all_gather(row_part, ("tp", "section")), axis=0)
     grad_tokens = (
         inv_rms[:, None] * own_gain * d_normed
         - own_inputs * (inv_rms**3 * row_sum / features)[:, None]

time: 197 us -> 189 us (0.959)
  blocking collectives: 77 us -> 68.4 us
    psum x1 -> x0, blocking collectives: 29.5 us -> none  [shards(): row_sum = lax.psum(row_part, ('tp', 'section'))]
    all_gather x0 -> x1, blocking collectives: none -> 20.9 us  [shards(): row_sum = jnp.sum(jax.lax.all_gather(row_part, ('tp', 'section')), axis=0)]
  transfers between devices with their start and end apart: 3 -> 3, of which waited for: 2 -> 2; matrix products, arithmetic and copies ran while one was open for 4% -> 5% of each run, Pallas kernels for 0% -> 0%
where the time goes in v1:
time: 189 us; the launch traced here: 188 us
  waiting for transfers between devices  72 us (38%)
  blocking collectives  68.4 us (36%)
  matrix products  15.4 us (8%)
  between operations  14.1 us (7%)
  local copies, waits for them, and re-layouts  9.56 us (5%)
  other arithmetic  6.93 us (4%)
    reduce_scatter x1, waiting for transfers between devices, shards(): lax.psum_scatter(d_part, ('tp', 'section'), scatter_dimension=0, tiled=True)  49.3 us
    all_gather x1, waiting for transfers between devices, shards(): d_all = lax.all_gather(d_both, 'dp', axis=0, tiled=True)  22.7 us
    all_gather x1, blocking collectives, shards(): row_sum = jnp.sum(jax.lax.all_gather(row_part, ('tp', 'section')), axis=0)  20.9 us
    all_to_all x1, blocking collectives, shards(): parts = lax.all_to_all(parts, 'dp', split_axis=0, concat_axis=0, tiled=True)  17.4 us
    all_to_all x1, blocking collectives, shards(): lax.all_to_all(normed, 'dp', split_axis=1, concat_axis=0, tiled=True)  13 us
    all_gather x1, blocking collectives, shards(): rows_in = lax.all_gather(tokens, 'section', axis=1, tiled=True)  9.38 us
    psum x1, blocking collectives, shards(): grad_gain = lax.psum(gain_part, 'dp')  7.8 us
    dot_general x1, matrix products, shards(): lax.dot_general(cols_normed, d_gate, contract_rows, preferred_element_typ...  3.79 us
  transfers between devices with their start and end apart: 3, of which 2 were waited for; matrix products, arithmetic and copies ran while one was open for 5% of the time, Pallas kernels for 0%

profile of v1, /device:TPU:0, one launch (start us, length us, event | category | flops | bytes accessed | tf_op | source)
XLA Modules:
  0.0 187.9 jit_solution(10869562676785284383)
XLA Ops:
  7.2 0.0 copy-start
  7.2 0.0 copy-start.5
  7.2 0.0 all-gather.4.cloned.1.call-start
  7.2 9.4 %all_gather.12 = bf16[128,2304]{0,1:T(8,128)(2,1)S(1)} all-gather(bf16[128,576]{0,1:T(8,128)(2,1)} %param.5), channel_id=1, replica_groups=mesh['dp'=2,'tp'=4,'section'=4] {'section'}, dimensions={1}, use_global_device_ids=true | all-gather | bytes 737280 | tf_op jit(solution)/shard_map/all_gather | solution.py:17
  16.6 0.3 multiply_reduce_fusion
  16.9 0.0 copy-done.5
  16.9 1.2 multiply_convert_fusion
  18.1 2.1 %copy.13 = bf16[128,2,1152]{2,0,1:T(8,128)(2,1)} copy(bf16[128,2,1152]{0,2,1:T(8,128)(2,1)} %bitcast.45) | data formatting | bytes 1179648 | tf_op jit(solution)/shard_map/all_to_all | solution.py:22
  20.3 13.0 %all_to_all.25 = bf16[128,2,1152]{2,0,1:T(8,128)(2,1)S(1)} all-to-all(bf16[128,2,1152]{2,0,1:T(8,128)(2,1)} %copy.13), channel_id=1, replica_groups=mesh['dp'=2,'tp'=4,'section'=4] {'dp'}, dimensions={1} | all-to-all | bytes 1179648 | tf_op jit(solution)/shard_map/all_to_all | solution.py:22
  33.2 0.0 copy-start.1
  33.2 3.0 %fusion.7 = bf16[2,128,1152]{2,1,0:T(8,128)(2,1)S(1)} fusion(bf16[1152,1152]{1,0:T(8,128)(2,1)} %param.9, bf16[128,2,1152]{2,0,1:T(8,128)(2,1)S(1)} %all_to_all.25), kind=kOutput, calls=%fused_computation.8 | convolution fusion | flops 679772160 | bytes 3833856 | tf_op jit(solution)/shard_map/dot_general | solution.py:25
  36.2 0.0 copy-done.1
  36.2 0.0 copy-done
  36.2 1.0 fusion.4
  37.2 0.1 pad_maximum_fusion
  37.3 17.4 %all_to_all.26 = bf16[2,128,2304]{2,1,0:T(8,128)(2,1)S(1)} all-to-all(bf16[2,128,2304]{2,1,0:T(8,128)(2,1)S(1)} %pad_maximum_fusion), channel_id=1, replica_groups=mesh['dp'=2,'tp'=4,'section'=4] {'dp'}, dimensions={0} | all-to-all | bytes 2359296 | tf_op jit(solution)/shard_map/all_to_all | solution.py:27
  54.7 0.0 copy-start.4
  54.7 0.2 convert_reduce_fusion
  54.9 0.8 copy-done.4
  55.7 0.5 fusion.19
  56.2 0.9 pad_maximum_fusion.1
  57.0 0.0 all-gather.4.cloned.1.call-update
  57.0 0.0 reduce-scatter.2.cloned.1.call-start
  57.1 22.7 %all-gather.4.cloned.1.call-done = bf16[256,2304]{1,0:T(8,128)(2,1)} async-done(((bf16[128,2304]{1,0:T(8,128)(2,1)}), bf16[256,2304]{1,0:T(8,128)(2,1)}) %all-gather.4.cloned.1.call-update) | async-done | bytes 1179664 | tf_op jit(solution)/shard_map/all_gather | solution.py:32
  79.8 0.0 copy-start.3
  79.8 0.0 copy-start.6
  79.8 2.2 %fusion.25 = f32[256,1152]{1,0:T(8,128)S(1)} fusion(bf16[1152,1152]{1,0:T(8,128)(2,1)S(1)} %copy-done, bf16[256,2304]{1,0:T(8,128)(2,1)} %all-gather.4.cloned.1.call-done), kind=kOutput, calls=%fused_computation.33 | convolution fusion | flops 679477248 | bytes 4423680 | tf_op jit(solution)/shard_map/dot_general | solution.py:36
  82.1 0.0 copy-done.3
  82.1 0.0 copy-done.6
  82.1 1.9 fusion.11
  84.0 2.1 %copy.14 = bf16[1152,256]{1,0:T(8,128)(2,1)} copy(bf16[1152,256]{0,1:T(8,128)(2,1)} %fusion.11) | data formatting | bytes 1179648 | tf_op jit(solution)/shard_map/convert_element_type | solution.py:40
  86.1 2.5 %reshape.42 = bf16[8,144,2,128]{3,2,1,0:T(2,128)(2,1)} reshape(bf16[1152,256]{1,0:T(8,128)(2,1)} %copy.14) | data formatting | bytes 1179648 | tf_op jit(solution)/shard_map/reshape | solution.py:41
  88.6 2.0 %copy.15 = bf16[2,8,144,128]{3,2,1,0:T(8,128)(2,1)} copy(bf16[2,8,144,128]{3,0,2,1:T(2,128)(2,1)} %bitcast.44) | data formatting | bytes 1179648 | tf_op jit(solution)/shard_map/transpose | solution.py:41
  90.5 0.0 reduce-scatter.2.cloned.1.call-update
  90.5 1.1 convert_element_type.31
  91.7 0.1 dynamic_slice.6
  91.7 0.0 copy-start.2
  91.7 3.8 %convolution_convert_fusion.1 = bf16[1152,1152]{1,0:T(8,128)(2,1)} fusion(bf16[256,1152]{1,0:T(8,128)(2,1)} %bitcast.41, bf16[256,2304]{1,0:T(8,128)(2,1)} %all-gather.4.cloned.1.call-done), kind=kOutput, calls=%fused_computation.1 | convolution fusion | flops 680804352 | bytes 3833856 | tf_op jit(solution)/shard_map/dot_general | solution.py:63
  95.5 49.3 %reduce-scatter.2.cloned.1.call-done = bf16[144,128]{1,0:T(8,128)(2,1)} async-done(((bf16[2304,128]{1,0:T(8,128)(2,1)}), bf16[144,128]{1,0:T(8,128)(2,1)}) %reduce-scatter.2.cloned.1.call-update) | async-done | bytes 36880 | tf_op jit(solution)/shard_map/reduce_scatter | solution.py:43
  144.8 1.4 collective-permute-start
  146.2 0.0 copy-done.2
  146.2 3.6 %convolution_convert_fusion = bf16[1152,1152]{1,0:T(8,128)(2,1)} fusion(bf16[256,1152]{1,0:T(8,128)(2,1)S(1)} %bitcast.42, bf16[256,2304]{1,0:T(8,128)(2,1)} %all-gather.4.cloned.1.call-done), kind=kOutput, calls=%fused_computation | convolution fusion | flops 680804352 | bytes 3833856 | tf_op jit(solution)/shard_map/dot_general | solution.py:66
  149.8 0.0 collective-permute-done
  149.8 1.0 fusion.31
  150.8 7.8 %psum.7 = f32[144]{0:T(256)} all-reduce(f32[144]{0:T(256)S(1)} %get-tuple-element.4), channel_id=1, replica_groups=mesh['dp'=2,'tp'=4,'section'=4] {'dp'}, use_global_device_ids=true, to_apply=%region_6.0 | all-reduce | flops 144 | bytes 1152 | tf_op jit(solution)/shard_map/psum | solution.py:57
  158.6 20.9 %all-gather.1 = f32[16,1,128]{2,1,0:T(1,128)S(1)} all-gather(f32[1,1,128]{2,1,0:T(1,128)S(1)} %bitcast.46), channel_id=2, replica_groups=mesh['dp'=2,'tp'=4,'section'=4] {'tp','section'}, dimensions={0}, use_global_device_ids=true | all-gather | bytes 8704 | tf_op jit(solution)/shard_map/all_gather | solution.py:58
  179.5 1.6 fusion.28
  (3 shorter events, 0.1 us)
Async XLA Ops:
  7.2 29.0 %copy-start = (bf16[1152,1152]{1,0:T(8,128)(2,1)S(1)}, bf16[1152,1152]{1,0:T(8,128)(2,1)}, u32[]{:S(2)}) copy-start(bf16[1152,1152]{1,0:T(8,128)(2,1)} %param.8) | copy-start | bytes 7962628
  7.2 9.8 %copy-start.5 = (f32[2304]{0:T(1024)S(1)}, f32[2304]{0:T(1024)}, u32[]{:S(2)}) copy-start(f32[2304]{0:T(1024)} %param.7) | copy-start | bytes 27652
  7.2 72.6 %all-gather.4.cloned.1.call-start = ((), (), s32[]{:S(2)}) async-start(), calls=%async_computation.3 | async-start | bytes 1769472 | tf_op jit(solution)/shard_map/all_gather | solution.py:32
  33.2 3.0 %copy-start.1 = (bf16[128,2,1152]{2,0,1:T(8,128)(2,1)}, bf16[128,2,1152]{2,0,1:T(8,128)(2,1)S(1)}, u32[]{:S(2)}) copy-start(bf16[128,2,1152]{2,0,1:T(8,128)(2,1)S(1)} %all_to_all.25) | copy-start | bytes 1769476
  54.7 1.0 copy-start.4
  57.0 87.8 %reduce-scatter.2.cloned.1.call-start = ((), (), s32[]{:S(2)}) async-start(), calls=%async_computation.4 | async-start | bytes 626688 | tf_op jit(solution)/shard_map/reduce_scatter | solution.py:43
  79.8 2.3 %copy-start.3 = (bf16[256,2304]{1,0:T(8,128)(2,1)S(1)}, bf16[256,2304]{1,0:T(8,128)(2,1)}, u32[]{:S(2)}) copy-start(bf16[256,2304]{1,0:T(8,128)(2,1)} %all-gather.4.cloned.1.call-done) | copy-start | bytes 3538948
  79.8 2.3 %copy-start.6 = (bf16[1152,1152]{1,0:T(8,128)(2,1)S(1)}, bf16[1152,1152]{1,0:T(8,128)(2,1)}, u32[]{:S(2)}) copy-start(bf16[1152,1152]{1,0:T(8,128)(2,1)} %param.9) | copy-start | bytes 7962628
  91.7 54.5 %copy-start.2 = (bf16[128,2,1152]{2,0,1:T(8,128)(2,1)S(1)}, bf16[128,2,1152]{2,0,1:T(8,128)(2,1)}, u32[]{:S(2)}) copy-start(bf16[128,2,1152]{2,0,1:T(8,128)(2,1)} %copy-done.1) | copy-start | bytes 1769476
  144.8 5.0 %collective-permute-start = (bf16[144,128]{1,0:T(8,128)(2,1)}, bf16[144,128]{1,0:T(8,128)(2,1)S(1)}, u32[]{:S(2)}, u32[]{:S(2)}) collective-permute-start(bf16[144,128]{1,0:T(8,128)(2,1)} %reduce-scatter.2.cloned.1.call-done), channel_id=1, source_target_pairs={{0,0},{1,1},{2,2},{3,3},{4,4},{5,5},{6,6},{7,7},{8,16},{9,17},{10,... | collective-permute-start | bytes 110600 | tf_op jit(solution)/shard_map/ppermute | solution.py:50
Sparse Core Ops, SparseCore 0:
  57.2 22.6 all-gather.3
  90.7 54.0 reduce-scatter.1
